TPU v7x, 32 devices: a whole 2x2x4 slice. The times are simulated.
32 devices in a mesh: grp: 2 (over y), slab: 4 (over z), head: 2 (over x), seq: 2 (over core).
Axes of the slice: x: 2, y: 2, z: 4, core: 2. Of those that a mesh axis runs over, the one named last changes fastest.
Arguments:
- queries: bfloat16 [1024, 5120], P(('grp', 'seq'), 'head'), parts along dimension 0, may hold values from -140 to 140
- query_gain: float32 [5120], P('head'), may hold values from 1.5 to 3
- cache_keys: bfloat16 [4096, 5120], P(('grp', 'slab'), 'head'), parts along dimension 0, may hold values from -120 to 120
- cache_values: bfloat16 [4096, 5120], P(('grp', 'slab'), 'head'), parts along dimension 0, may hold values from -6 to 6
- finished_keys: bfloat16 [1024, 5120], P(('grp', 'slab', 'seq'), 'head'), parts along dimension 0, may hold values from -6 to 6
- finished_values: bfloat16 [1024, 5120], P(('grp', 'slab', 'seq'), 'head'), parts along dimension 0, may hold values from -6 to 6
- new_keys: bfloat16 [1024, 5120], P(('grp', 'slab', 'seq'), 'head'), parts along dimension 0, may hold values from -6 to 6
- new_values: bfloat16 [1024, 5120], P(('grp', 'slab', 'seq'), 'head'), parts along dimension 0, may hold values from -6 to 6
- out_weight: bfloat16 [5120, 5120], P('head', 'slab'), may hold values from -0.25 to 0.25
- time_weight: float32 [256, 5120], P(None, ('slab', 'head')), may hold values from -0.375 to 0.375
- owner: int32 [2], P('grp'), parts along dimension 0, may hold values from 0 to 3
- step: int32 [2], P('grp'), parts along dimension 0, may hold values from 0 to 999
Outputs:
- branch: bfloat16 [1024, 5120], P(('grp', 'seq'), ('slab', 'head')), parts along dimension 0
There are 2 independent parts, one for each index of `grp`. A program takes and returns all parts, laid end to end along the dimension named above; an argument that names none is the same for every part. Nothing has to cross between parts.
All inputs are finite; a program needn't handle non-finite values.
Results may differ from a plain program's by a relative error of at most 0.012.
Values may be sent and summed in bfloat16 or wider, within the bound.
A program may use at most 64 MiB of HBM per device.

v0:
```python
from functools import reduce

import jax
import jax.numpy as jnp
from jax import lax
from jax.sharding import PartitionSpec as P

HEADS = 40
HD = 128


EPSILON = 1e-06


def local(
    queries,
    query_gain,
    cache_keys,
    cache_values,
    finished_keys,
    finished_values,
    new_keys,
    new_values,
    out_weight,
    time_weight,
    owner,
    step,
):
    row_count = queries.shape[0]
    head_count = queries.shape[1] // HD
    query_float = queries.astype(jnp.float32)
    norm_total = lax.psum(jnp.sum(query_float * query_float, axis=1), "head")
    inverse = lax.rsqrt(norm_total / (HEADS * HD) + EPSILON)
    normed = (
        (query_float * inverse[:, None] * query_gain)
        .astype(jnp.bfloat16)
        .reshape(row_count, head_count, HD)
    )
    is_owner = lax.axis_index("slab") == owner[0]
    whole_keys, whole_values = (
        lax.all_gather(finished_keys, ("slab", "seq"), axis=0, tiled=True),
        lax.all_gather(finished_values, ("slab", "seq"), axis=0, tiled=True),
    )
    fresh_keys, fresh_values = (
        lax.all_gather(new_keys, "seq", axis=0, tiled=True),
        lax.all_gather(new_values, "seq", axis=0, tiled=True),
    )
    key_block = jnp.where(is_owner, whole_keys, cache_keys)
    value_block = jnp.where(is_owner, whole_values, cache_values)
    blocks = [
        (key_block, value_block, jnp.float32(0.0)),
        (fresh_keys, fresh_values, jnp.float32(0.0)),
    ]
    score_scale = 1.0 / HD**0.5
    score_list = []
    for key_block, value_block, penalty in blocks:
        key_heads = key_block.reshape(key_block.shape[0], head_count, HD)
        each_score = jnp.einsum(
            "rhd,khd->hrk", normed, key_heads, preferred_element_type=jnp.float32
        )
        score_list.append(each_score * score_scale)
    row_top = reduce(jnp.maximum, [jnp.max(each_score, axis=2) for each_score in score_list])
    row_mass = jnp.zeros_like(row_top)
    partial_value = jnp.zeros((head_count, row_count, HD), jnp.float32)
    for each_score, (key_block, value_block, penalty) in zip(score_list, blocks):
        raw_weights = jnp.exp(each_score - row_top[:, :, None])
        row_mass = row_mass + jnp.sum(raw_weights, axis=2)
        value_heads = value_block.reshape(value_block.shape[0], head_count, HD)
        partial_value = partial_value + jnp.einsum(
            "hrk,khd->hrd",
            raw_weights.astype(jnp.bfloat16),
            value_heads,
            preferred_element_type=jnp.float32,
        )
    global_top = lax.pmax(row_top, "slab")
    factor = jnp.exp(row_top - global_top)
    sum_share, mass_share = (
        lax.psum_scatter(
            partial_value * factor[:, :, None], "slab", scatter_dimension=1, tiled=True
        ),
        lax.psum_scatter(row_mass * factor, "slab", scatter_dimension=1, tiled=True),
    )
    row_share = (sum_share / mass_share[:, :, None]).astype(jnp.bfloat16)
    attended = lax.all_gather(row_share, "slab", axis=1, tiled=True)
    weight_heads = out_weight.reshape(head_count, HD, out_weight.shape[1])
    projected = jnp.einsum(
        "hrd,hdc->rc", attended, weight_heads, preferred_element_type=jnp.float32
    )
    summed = lax.psum_scatter(projected, "head", scatter_dimension=1, tiled=True)
    half = time_weight.shape[0] // 2
    frequency = jnp.exp(-jnp.log(10000.0) * jnp.arange(half, dtype=jnp.float32) / half)
    phases = step[0].astype(jnp.float32) * frequency
    embedding = jnp.concatenate([jnp.cos(phases), jnp.sin(phases)])
    time_gate = 1.0 + jnp.dot(embedding, time_weight, precision=lax.Precision.HIGHEST)
    return (time_gate * summed).astype(jnp.bfloat16)


def solution(mesh):
    in_specs = (
        P(("grp", "seq"), "head"),
        P("head"),
        P(("grp", "slab"), "head"),
        P(("grp", "slab"), "head"),
        P(("grp", "slab", "seq"), "head"),
        P(("grp", "slab", "seq"), "head"),
        P(("grp", "slab", "seq"), "head"),
        P(("grp", "slab", "seq"), "head"),
        P("head", "slab"),
        P(None, ("slab", "head")),
        P("grp"),
        P("grp"),
    )
    out_specs = P(("grp", "seq"), ("slab", "head"))
    return jax.shard_map(local, mesh=mesh, in_specs=in_specs, out_specs=out_specs, check_vma=False)
```

profile of v0, /device:TPU:0, one launch (start us, length us, event | category | flops | bytes accessed | tf_op | source)
XLA Modules:
  0.0 240.0 jit_solution(8406601955525841598)
XLA Ops:
  6.5 0.0 all-gather.4.cloned.1.call-start
  6.5 0.7 all-gather.4.cloned.1.call-update
  7.3 0.0 all-gather.6.cloned.1.call-start
  7.3 0.7 all-gather.6.cloned.1.call-update
  8.0 0.0 reduce-scatter.10.cloned.1.call-start
  8.1 4.5 %copy.36 = bf16[512,2560]{0,1:T(8,128)(2,1)} copy(bf16[512,2560]{1,0:T(8,128)(2,1)} %param.15) | data formatting | bytes 5242880 | tf_op args[3]
  13.3 0.6 copy.27
  13.9 0.0 copy-start.4
  13.9 0.0 copy-start.5
  13.9 4.5 %copy.29 = bf16[512,2560]{0,1:T(8,128)(2,1)} copy(bf16[512,2560]{1,0:T(8,128)(2,1)} %param.14) | data formatting | bytes 5242880 | tf_op args[2]
  18.4 2.7 %all_gather.16 = bf16[128,2560]{1,0:T(8,128)(2,1)S(1)} all-gather(bf16[64,2560]{1,0:T(8,128)(2,1)S(1)} %copy-done.4), channel_id=1, replica_groups=mesh['grp'=2,'slab'=4,'head'=2,'seq'=2] {'seq'}, dimensions={0}, use_global_device_ids=true | all-gather | bytes 983040 | tf_op jit(solution)/shard_map/all_gather | solution.py:45
  21.1 1.1 copy.32
  22.2 2.3 all_gather.18
  24.4 1.1 copy.38
  25.5 0.4 fusion.6
  25.9 5.5 %psum.7 = f32[256]{0:T(256)S(1)} all-reduce(f32[256]{0:T(256)S(1)} %fusion.6), channel_id=1, replica_groups=mesh['grp'=2,'slab'=4,'head'=2,'seq'=2] {'head'}, use_global_device_ids=true, to_apply=%region_1.0 | all-reduce | flops 256 | bytes 2048 | tf_op jit(solution)/shard_map/psum | solution.py:32
  31.5 0.4 fusion.8
  31.9 1.2 copy-done.1
  33.0 1.7 multiply_reduce_fusion.1
  34.7 10.7 %all-gather.4.cloned.1.call-done = bf16[512,2560]{1,0:T(8,128)(2,1)} async-done(((bf16[64,2560]{1,0:T(8,128)(2,1)}), bf16[512,2560]{1,0:T(8,128)(2,1)}) %all-gather.4.cloned.1.call-update) | async-done | bytes 2621456 | tf_op jit(solution)/shard_map/all_gather | solution.py:41
  45.4 4.4 %copy.28 = bf16[512,2560]{0,1:T(8,128)(2,1)} copy(bf16[512,2560]{1,0:T(8,128)(2,1)} %all-gather.4.cloned.1.call-done) | data formatting | bytes 5242880 | tf_op jit(solution)/shard_map/all_gather | solution.py:41
  49.8 2.1 broadcast_select_fusion.1
  52.0 5.7 %multiply_reduce_fusion = (f32[20,256]{1,0:T(8,128)S(1)}, f32[20,256,512]{2,1,0:T(8,128)}) fusion(bf16[256,20,128]{0,2,1:T(8,128)(2,1)S(1)} %bitcast.25, bf16[512,20,128]{0,2,1:T(8,128)(2,1)S(1)} %bitcast.27), kind=kOutput, calls=%fused_computation.1 | convolution fusion | flops 676326400 | bytes 14438400 | tf_op jit(solution)/shard_map/rhd,khd->hrk/dot_general | solution.py:58
  57.6 18.7 %pmax.7 = f32[20,256]{1,0:T(8,128)S(1)} all-reduce(f32[20,256]{1,0:T(8,128)S(1)} %max.9), channel_id=1, replica_groups=mesh['grp'=2,'slab'=4,'head'=2,'seq'=2] {'slab'}, use_global_device_ids=true, to_apply=%region_4.5 | all-reduce | flops 5120 | bytes 40960 | tf_op jit(solution)/shard_map/pmax | solution.py:75
  76.4 5.9 %fusion = f32[20,256]{1,0:T(8,128)S(1)} fusion(f32[20,256,512]{2,1,0:T(8,128)} %get-tuple-element.8, f32[20,256]{1,0:T(8,128)S(1)} %max.9), kind=kLoop, calls=%fused_computation.2 | loop fusion | flops 7859200 | bytes 10526720 | tf_op jit(solution)/shard_map/reduce_sum | solution.py:67
  82.2 0.0 all-gather.6.cloned.1.call-done
  82.3 4.4 %copy.35 = bf16[512,2560]{0,1:T(8,128)(2,1)} copy(bf16[512,2560]{1,0:T(8,128)(2,1)} %all-gather.6.cloned.1.call-done) | data formatting | bytes 5242880 | tf_op jit(solution)/shard_map/all_gather | solution.py:42
  86.7 2.0 broadcast_select_fusion
  88.7 7.7 %fusion.2 = f32[20,256,128]{2,1,0:T(8,128)} fusion(bf16[512,20,128]{0,2,1:T(8,128)(2,1)S(1)} %bitcast.26, f32[20,256,512]{2,1,0:T(8,128)} %get-tuple-element.8, f32[20,256]{1,0:T(8,128)S(1)} %max.9), kind=kOutput, calls=%fused_computation.4 | convolution fusion | flops 678952960 | bytes 15749120 | tf_op jit(solution)/shard_map/hrk,khd->hrd/dot_general | solution.py:69
  96.4 0.5 fusion.9
  96.9 0.8 copy.48
  97.6 0.0 reduce-scatter.10.cloned.1.call-update
  97.7 0.0 reduce-scatter.6.cloned.1.call-start
  97.7 4.1 %add_multiply_fusion = f32[20,256,128]{2,1,0:T(8,128)} fusion(f32[20,256,128]{2,1,0:T(8,128)} %fusion.2, bf16[128,20,128]{0,2,1:T(8,128)(2,1)} %bitcast.28, f32[20,256,128]{1,2,0:T(8,128)S(1)} %get-tuple-element.10, f32[20,256]{1,0:T(8,128)S(1)} %get-tuple-element.6, f32[20,256]{1,0:T(8,128)S(1)} %max.9), kind=kOutput, calls=%fused_computation.13 | convolution fusion | flops 171048960 | bytes 8560640 | tf_op jit(solution)/shard_map/hrk,khd->hrd/dot_general | solution.py:69
  101.8 0.0 reduce-scatter.6.cloned.1.call-update
  101.8 0.0 all-gather.8.cloned.1.call-start
  101.9 13.7 %reduce-scatter.10.cloned.1.call-done = f32[64,20]{1,0:T(8,128)} async-done(((f32[256,20]{1,0:T(8,128)}), f32[64,20]{1,0:T(8,128)}) %reduce-scatter.10.cloned.1.call-update) | async-done | bytes 5136
  115.6 0.8 copy.49
  116.5 51.8 %reduce-scatter.6.cloned.1.call-done = f32[20,64,128]{2,1,0:T(8,128)} async-done(((f32[20,256,128]{2,1,0:T(8,128)}), f32[20,64,128]{2,1,0:T(8,128)}) %reduce-scatter.6.cloned.1.call-update) | async-done | bytes 655376 | tf_op jit(solution)/shard_map/reduce_scatter | solution.py:78
  168.2 2.1 divide_convert_fusion
  170.3 0.0 all-gather.8.cloned.1.call-update
  170.3 0.0 reduce-scatter.8.cloned.1.call-start
  170.4 32.2 %all-gather.8.cloned.1.call-done = bf16[20,256,128]{2,1,0:T(8,128)(2,1)} async-done(((bf16[20,64,128]{2,1,0:T(8,128)(2,1)}), bf16[20,256,128]{2,1,0:T(8,128)(2,1)}) %all-gather.8.cloned.1.call-update) | async-done | bytes 1310736 | tf_op jit(solution)/shard_map/all_gather | solution.py:84
  202.5 6.2 %convolution_bitcast_fusion = f32[256,1280]{1,0:T(8,128)} fusion(bf16[20,256,128]{2,1,0:T(8,128)(2,1)} %all-gather.8.cloned.1.call-done, bf16[20,128,1280]{2,1,0:T(8,128)(2,1)} %bitcast.33), kind=kOutput, calls=%fused_computation.9 | convolution fusion | flops 1677721600 | bytes 9175040 | tf_op jit(solution)/shard_map/hrd,hdc->rc/dot_general | solution.py:86
  208.7 0.0 reduce-scatter.8.cloned.1.call-update
  209.5 0.4 convolution_reduce_fusion
  209.9 21.4 %reduce-scatter.8.cloned.1.call-done = f32[256,640]{1,0:T(8,128)} async-done(((f32[256,1280]{1,0:T(8,128)}), f32[256,640]{1,0:T(8,128)}) %reduce-scatter.8.cloned.1.call-update) | async-done | bytes 655376 | tf_op jit(solution)/shard_map/reduce_scatter | solution.py:89
  231.3 1.9 multiply_convert_fusion
  (17 shorter events, 0.1 us)
Async XLA Ops:
  6.5 202.9 %copy-start = (f32[256,640]{1,0:T(8,128)S(1)}, f32[256,640]{1,0:T(8,128)}, u32[]{:S(2)}) copy-start(f32[256,640]{1,0:T(8,128)} %param.21) | copy-start | bytes 1966084
  6.5 38.9 %all-gather.4.cloned.1.call-start = ((), (), s32[]{:S(2)}) async-start(), calls=%async_computation.3 | async-start | bytes 2949120 | tf_op jit(solution)/shard_map/all_gather | solution.py:41
  7.3 75.0 %all-gather.6.cloned.1.call-start = ((), (), s32[]{:S(2)}) async-start(), calls=%async_computation.4 | async-start | bytes 2949120 | tf_op jit(solution)/shard_map/all_gather | solution.py:42
  8.0 107.6 %reduce-scatter.10.cloned.1.call-start = ((), (), s32[]{:S(2)}) async-start(), calls=%async_computation.8 | async-start | bytes 163840
  8.1 5.2 %copy-start.3 = (bf16[256,2560]{1,0:T(8,128)(2,1)S(1)}, bf16[256,2560]{1,0:T(8,128)(2,1)}, u32[]{:S(2)}) copy-start(bf16[256,2560]{1,0:T(8,128)(2,1)} %param.12) | copy-start | bytes 3932164
  13.9 4.5 %copy-start.4 = (bf16[64,2560]{1,0:T(8,128)(2,1)S(1)}, bf16[64,2560]{1,0:T(8,128)(2,1)}, u32[]{:S(2)}) copy-start(bf16[64,2560]{1,0:T(8,128)(2,1)} %param.18) | copy-start | bytes 983044
  13.9 8.3 %copy-start.5 = (bf16[64,2560]{1,0:T(8,128)(2,1)S(1)}, bf16[64,2560]{1,0:T(8,128)(2,1)}, u32[]{:S(2)}) copy-start(bf16[64,2560]{1,0:T(8,128)(2,1)} %param.19) | copy-start | bytes 983044
  21.1 10.4 %copy-start.6 = (f32[2560]{0:T(1024)S(1)}, f32[2560]{0:T(1024)}, u32[]{:S(2)}) copy-start(f32[2560]{0:T(1024)} %param.13) | copy-start | bytes 30724
  31.9 1.2 copy-start.1
  49.8 2.1 copy-start.2
  97.7 70.6 %reduce-scatter.6.cloned.1.call-start = ((), (), s32[]{:S(2)}) async-start(), calls=%async_computation.5 | async-start | bytes 3276800 | tf_op jit(solution)/shard_map/reduce_scatter | solution.py:78
  101.8 100.7 %all-gather.8.cloned.1.call-start = ((), (), s32[]{:S(2)}) async-start(), calls=%async_computation.6 | async-start | bytes 1638400 | tf_op jit(solution)/shard_map/all_gather | solution.py:84
  170.3 61.0 %reduce-scatter.8.cloned.1.call-start = ((), (), s32[]{:S(2)}) async-start(), calls=%async_computation.7 | async-start | bytes 1966080 | tf_op jit(solution)/shard_map/reduce_scatter | solution.py:89
Sparse Core Ops, SparseCore 0:
  9.0 36.4 all-gather.3
  47.1 33.8 all-gather.5
  97.8 17.7 reduce-scatter.9
  117.8 50.4 reduce-scatter.5
  170.4 32.0 all-gather.7
  208.9 22.3 reduce-scatter.7
where the time goes:
time: 241 us; the launch traced here: 240 us
  waiting for transfers between devices  131 us (54%)
  blocking collectives  29.2 us (12%)
  matrix products  25.7 us (11%)
  local copies, waits for them, and re-layouts  23.4 us (10%)
  other arithmetic  15.2 us (6%)
  between operations  14.9 us (6%)
    reduce_scatter x1, waiting for transfers between devices, local(): lax.psum_scatter(partial_value * factor[:, :, None], 'slab', scatter_dime...  51.8 us
    all_gather x1, waiting for transfers between devices, local(): attended = lax.all_gather(row_share, 'slab', axis=1, tiled=True)  32.2 us
    reduce_scatter x1, waiting for transfers between devices, local(): lax.psum_scatter(projected, 'head', scatter_dimension=1, tiled=True)  21.4 us
    pmax x1, blocking collectives, local(): global_top = lax.pmax(row_top, 'slab')  18.7 us
    unnamed x7, waiting for transfers between devices  15.2 us
    unnamed x19, local copies, waits for them, and re-layouts  12.4 us
    dot_general x2, matrix products, local(): jnp.einsum('hrk,khd->hrd', raw_weights.astype(jnp.bfloat16), value_heads,...  11.8 us
    all_gather x1, waiting for transfers between devices, local(): lax.all_gather(finished_keys, ('slab', 'seq'), axis=0, tiled=True)  10.7 us
  transfers between devices with their start and end apart: 6, of which 5 were waited for; matrix products, arithmetic and copies ran while one was open for 16% of the time, Pallas kernels for 0%

commit v1 on v0

v1 whole, which is shorter than its diff:
```python
import functools
import math

import jax
import jax.numpy as jnp
from jax import lax
from jax.experimental import pallas as pl
from jax.experimental.pallas import tpu as pltpu
from jax.sharding import PartitionSpec as P

HEADS = 40
HD = 128
EPSILON = 1e-06
LOW = -1e30
LAG = 3
MESH = pl.DeviceIdType.MESH
F32 = jnp.float32
BF16 = jnp.bfloat16


def kernel(
    dims,
    aligned,
    q_ref,
    gain_ref,
    ck_ref,
    cv_ref,
    fk_ref,
    fv_ref,
    nk_ref,
    nv_ref,
    w_ref,
    tw_ref,
    owner_ref,
    step_ref,
    out_ref,
    q,
    qg,
    gain,
    kc,
    vc,
    kf,
    vf,
    w,
    tw,
    squares,
    scale,
    own_o,
    own_s,
    pre_o,
    pre_s,
    suf_o,
    suf_s,
    right_o,
    right_s,
    left_o,
    left_s,
    acc,
    gate,
    xs,
    xr,
    load_sem,
    fresh_sem,
    fresh_send,
    fresh_recv,
    sq_send,
    sq_recv,
    right_send,
    right_recv,
    left_send,
    left_recv,
    x_send,
    x_recv,
):
    n, heads_n, seq_n = dims
    rows, width = q_ref.shape
    hcount = width // HD
    z = lax.axis_index("slab")
    hx = lax.axis_index("head")
    sq = lax.axis_index("seq")

    loads = [
        pltpu.make_async_copy(src, dst, load_sem.at[i])
        for i, (src, dst) in enumerate(
            [(q_ref, q), (gain_ref, gain), (ck_ref, kc), (cv_ref, vc), (w_ref, w), (tw_ref, tw)]
        )
    ]
    for c in loads:
        c.start()
    fresh_src = [(fk_ref, kf, 0), (nk_ref, kf, 1), (fv_ref, vf, 0), (nv_ref, vf, 1)]
    fresh_local = []
    for i, (src, dst, part) in enumerate(fresh_src):
        c = pltpu.make_async_copy(src, dst.at[sq, part], fresh_sem.at[i])
        c.start()
        fresh_local.append(c)

    barrier = pltpu.get_barrier_semaphore()
    for d in range(1, seq_n):
        pl.semaphore_signal(
            barrier, inc=1, device_id={"seq": lax.rem(sq + d, seq_n)}, device_id_type=MESH
        )
    for d in range(1, heads_n):
        pl.semaphore_signal(
            barrier, inc=1, device_id={"head": lax.rem(hx + d, heads_n)}, device_id_type=MESH
        )

    @pl.when(z > 0)
    def _():
        pl.semaphore_signal(barrier, inc=1, device_id={"slab": z - 1}, device_id_type=MESH)

    @pl.when(z < n - 1)
    def _():
        pl.semaphore_signal(barrier, inc=1, device_id={"slab": z + 1}, device_id_type=MESH)

    ends = (z == 0).astype(jnp.int32) + (z == n - 1).astype(jnp.int32)
    pl.semaphore_wait(barrier, seq_n - 1 + heads_n - 1 + 2 - ends)

    fresh_remote = []
    for d in range(1, seq_n):
        for i, (src, dst, part) in enumerate(fresh_src):
            c = pltpu.make_async_remote_copy(
                src_ref=src,
                dst_ref=dst.at[sq, part],
                send_sem=fresh_send.at[d - 1, i],
                recv_sem=fresh_recv.at[d - 1, i],
                device_id={"seq": lax.rem(sq + d, seq_n)},
                device_id_type=MESH,
            )
            c.start()
            fresh_remote.append(c)

    loads[0].wait()
    loads[1].wait()

    def squares_step(h, total):
        cols = pl.ds(pl.multiple_of(h * HD, HD), HD)
        x = q[:, cols].astype(F32)
        qg[:, cols] = (x * gain[:, cols]).astype(BF16)
        return total + x * x

    total = lax.fori_loop(0, hcount, squares_step, jnp.zeros((rows, HD), F32))
    row_total = jnp.sum(total.T, axis=0, keepdims=True)
    squares[hx] = jnp.broadcast_to(row_total, (8, rows))
    loads[2].wait()
    loads[3].wait()
    sq_copies = []
    for d in range(1, heads_n):
        c = pltpu.make_async_remote_copy(
            src_ref=squares.at[hx],
            dst_ref=squares.at[hx],
            send_sem=sq_send.at[d - 1],
            recv_sem=sq_recv.at[d - 1],
            device_id={"head": lax.rem(hx + d, heads_n)},
            device_id_type=MESH,
        )
        c.start()
        sq_copies.append(c)
    for c in fresh_local:
        c.wait()
    for c in fresh_remote:
        c.wait_recv()
    for c in sq_copies:
        c.wait_recv()
    norm_total = jnp.sum(squares[...], axis=0)
    scale[...] = lax.rsqrt(norm_total / (HEADS * HD) + EPSILON) * (
        math.log2(math.e) / HD**0.5
    )
    loads[4].wait()
    loads[5].wait()

    def send(h, direction):
        if direction > 0:
            pairs, ss, rs = ((right_o, pre_o), (right_s, pre_s)), right_send, right_recv
        else:
            pairs, ss, rs = ((left_o, suf_o), (left_s, suf_s)), left_send, left_recv
        return [
            pltpu.make_async_remote_copy(
                src_ref=src.at[h],
                dst_ref=dst.at[h],
                send_sem=ss.at[h, i],
                recv_sem=rs.at[h, i],
                device_id={"slab": z + direction},
                device_id_type=MESH,
            )
            for i, (src, dst) in enumerate(pairs)
        ]

    @pl.when(z == 0)
    def _():
        pre_o[...] = jnp.zeros_like(pre_o)
        pre_s[:, 0:1, :] = jnp.full((hcount, 1, rows), LOW, F32)
        pre_s[:, 1:2, :] = jnp.zeros((hcount, 1, rows), F32)

    @pl.when(z == n - 1)
    def _():
        suf_o[...] = jnp.zeros_like(suf_o)
        suf_s[:, 0:1, :] = jnp.full((hcount, 1, rows), LOW, F32)
        suf_s[:, 1:2, :] = jnp.zeros((hcount, 1, rows), F32)

    fresh_rows = seq_n * 2 * fk_ref.shape[0]
    lag_end = LAG * jnp.maximum(z, n - 1 - z)

    def combine(h, other_o, other_s, dest_o, dest_s):
        m_a, l_a = own_s[h, 0:1], own_s[h, 1:2]
        m_b, l_b = other_s[h, 0:1], other_s[h, 1:2]
        top = jnp.maximum(m_a, m_b)
        e_a, e_b = jnp.exp2(m_a - top), jnp.exp2(m_b - top)
        dest_o[h] = (own_o[h] * e_a + other_o[h].astype(F32) * e_b).astype(BF16)
        dest_s[h, 0:1] = top
        dest_s[h, 1:2] = l_a * e_a + l_b * e_b

    def body(t, carry):
        @pl.when(t < hcount)
        def _():
            h = t
            cols = pl.ds(pl.multiple_of(h * HD, HD), HD)
            penalty = jnp.where(
                jnp.full((1, rows), owner_ref[0], jnp.int32) == z, F32(LOW), F32(0.0)
            )
            q_head = qg[:, cols]
            s_row = scale[0:1]
            nt = (((1,), (1,)), ((), ()))
            tn = (((0,), (0,)), ((), ()))
            s_c = (
                lax.dot_general(kc[:, cols], q_head, nt, preferred_element_type=F32) * s_row
                + penalty
            )
            k_fresh = kf[:, :, :, cols].reshape(fresh_rows, HD)
            v_fresh = vf[:, :, :, cols].reshape(fresh_rows, HD)
            s_f = lax.dot_general(k_fresh, q_head, nt, preferred_element_type=F32) * s_row
            top = jnp.maximum(
                jnp.max(s_c, axis=0, keepdims=True), jnp.max(s_f, axis=0, keepdims=True)
            )
            p_c = jnp.exp2(s_c - top)
            p_f = jnp.exp2(s_f - top)
            own_s[h, 0:1] = top
            own_s[h, 1:2] = jnp.sum(p_c, axis=0, keepdims=True) + jnp.sum(
                p_f, axis=0, keepdims=True
            )
            own_o[h] = lax.dot_general(
                vc[:, cols], p_c.astype(BF16), tn, preferred_element_type=F32
            ) + lax.dot_general(v_fresh, p_f.astype(BF16), tn, preferred_element_type=F32)

        hp = t - LAG * z
        in_p = (hp >= 0) & (hp < hcount)
        hs = t - LAG * (n - 1 - z)
        in_s = (hs >= 0) & (hs < hcount)

        @pl.when(in_p & (z > 0))
        def _():
            for c in send(hp, 1):
                c.wait_recv()

        @pl.when(in_p & (z < n - 1))
        def _():
            combine(hp, pre_o, pre_s, right_o, right_s)

        @pl.when(in_s & (z < n - 1))
        def _():
            for c in send(hs, -1):
                c.wait_recv()

        @pl.when(in_s & (z > 0))
        def _():
            combine(hs, suf_o, suf_s, left_o, left_s)

        @pl.when(in_p & (z < n - 1))
        def _():
            for c in send(hp, 1):
                c.start()

        @pl.when(in_s & (z > 0))
        def _():
            for c in send(hs, -1):
                c.start()

        if aligned:

            @pl.when(t == hcount - 1)
            def _():
                half = tw.shape[0] // 2
                j = lax.broadcasted_iota(jnp.int32, (half, HD), 0).astype(F32)
                frequency = jnp.exp(F32(-math.log(10000.0)) * j / half)
                phases = jnp.full((half, HD), step_ref[0], jnp.int32).astype(F32) * frequency
                cos, sin = jnp.cos(phases), jnp.sin(phases)
                for c in range(tw.shape[1] // HD):
                    cols = slice(c * HD, (c + 1) * HD)
                    terms = tw[:half, cols] * cos + tw[half:, cols] * sin
                    gate[:, cols] = 1.0 + jnp.sum(terms, axis=0, keepdims=True)

        hf = t - lag_end

        @pl.when((hf >= 0) & (hf < hcount))
        def _():
            h = hf
            m_a, m_b, m_c = own_s[h, 0:1], pre_s[h, 0:1], suf_s[h, 0:1]
            top = jnp.maximum(m_a, jnp.maximum(m_b, m_c))
            e_a, e_b, e_c = jnp.exp2(m_a - top), jnp.exp2(m_b - top), jnp.exp2(m_c - top)
            mass = own_s[h, 1:2] * e_a + pre_s[h, 1:2] * e_b + suf_s[h, 1:2] * e_c
            total_o = (
                own_o[h] * e_a + pre_o[h].astype(F32) * e_b + suf_o[h].astype(F32) * e_c
            )
            attended = (total_o / mass).astype(BF16)
            term = lax.dot_general(
                attended,
                w[pl.ds(pl.multiple_of(h * HD, HD), HD), :],
                (((0,), (0,)), ((), ())),
                preferred_element_type=F32,
            )

            @pl.when(h == 0)
            def _():
                acc[...] = term

            @pl.when(h > 0)
            def _():
                acc[...] += term

        return carry

    lax.fori_loop(0, hcount + LAG * (n - 1), body, 0)

    if aligned:
        cp = out_ref.shape[1]
        blocks = x_send.shape[1]
        block = rows // blocks
        x_copies = []
        for b in range(blocks):
            part = slice(b * block, (b + 1) * block)
            for d in range(1, heads_n):
                peer = lax.rem(hx + d, heads_n)
                cols = pl.ds(pl.multiple_of(peer * cp, HD), cp)
                xs[d - 1, b] = acc[part, cols].astype(BF16)
                c = pltpu.make_async_remote_copy(
                    src_ref=xs.at[d - 1, b],
                    dst_ref=xr.at[d - 1, b],
                    send_sem=x_send.at[d - 1, b],
                    recv_sem=x_recv.at[d - 1, b],
                    device_id={"head": peer},
                    device_id_type=MESH,
                )
                c.start()
                x_copies.append((b, d, c))
        mine = pl.ds(pl.multiple_of(hx * cp, HD), cp)
        for b in range(blocks):
            part = slice(b * block, (b + 1) * block)
            summed = acc[part, mine]
            for bb, d, c in x_copies:
                if bb == b:
                    c.wait_recv()
                    summed = summed + xr[d - 1, b].astype(F32)
            out_ref[part, :] = (summed * gate[0:1]).astype(out_ref.dtype)
        for b, d, c in x_copies:
            c.wait_send()
    else:
        out_ref[...] = acc[...]

    for c in fresh_remote + sq_copies:
        c.wait_send()

    def drain(h, carry):
        @pl.when(z < n - 1)
        def _():
            for c in send(h, 1):
                c.wait_send()

        @pl.when(z > 0)
        def _():
            for c in send(h, -1):
                c.wait_send()

        return carry

    lax.fori_loop(0, hcount, drain, 0)


def local(sizes, *args):
    (
        queries,
        query_gain,
        cache_keys,
        cache_values,
        finished_keys,
        finished_values,
        new_keys,
        new_values,
        out_weight,
        time_weight,
        owner,
        step,
    ) = args
    n, heads_n, seq_n = sizes
    rows, width = queries.shape
    hcount = width // HD
    cached, fresh = cache_keys.shape[0], finished_keys.shape[0]
    columns, cp = out_weight.shape[1], time_weight.shape[1]
    freq = time_weight.shape[0]
    aligned = cp % HD == 0
    blocks = 4
    any_spec = pl.BlockSpec(memory_space=pl.ANY)
    smem = pl.BlockSpec(memory_space=pltpu.SMEM)
    vmem = pl.BlockSpec(memory_space=pltpu.VMEM)
    dma = pltpu.SemaphoreType.DMA
    xcount = max(heads_n - 1, 1)
    stat = (hcount, 2, rows)
    part = (hcount, HD, rows)
    result = pl.pallas_call(
        functools.partial(kernel, sizes, aligned),
        out_shape=jax.ShapeDtypeStruct(
            (rows, cp if aligned else columns), BF16 if aligned else F32
        ),
        in_specs=[any_spec] * 10 + [smem] * 2,
        out_specs=vmem,
        scratch_shapes=[
            pltpu.VMEM((rows, width), BF16),
            pltpu.VMEM((rows, width), BF16),
            pltpu.VMEM((1, width), F32),
            pltpu.VMEM((cached, width), BF16),
            pltpu.VMEM((cached, width), BF16),
            pltpu.VMEM((seq_n, 2, fresh, width), BF16),
            pltpu.VMEM((seq_n, 2, fresh, width), BF16),
            pltpu.VMEM((width, columns), BF16),
            pltpu.VMEM((freq, cp), F32),
            pltpu.VMEM((heads_n, 8, rows), F32),
            pltpu.VMEM((8, rows), F32),
            pltpu.VMEM(part, F32),
            pltpu.VMEM(stat, F32),
            pltpu.VMEM(part, BF16),
            pltpu.VMEM(stat, F32),
            pltpu.VMEM(part, BF16),
            pltpu.VMEM(stat, F32),
            pltpu.VMEM(part, BF16),
            pltpu.VMEM(stat, F32),
            pltpu.VMEM(part, BF16),
            pltpu.VMEM(stat, F32),
            pltpu.VMEM((rows, columns), F32),
            pltpu.VMEM((1, cp), F32),
            pltpu.VMEM((xcount, blocks, rows // blocks, cp), BF16),
            pltpu.VMEM((xcount, blocks, rows // blocks, cp), BF16),
            dma((6,)),
            dma((4,)),
            dma((max(seq_n - 1, 1), 4)),
            dma((max(seq_n - 1, 1), 4)),
            dma((xcount,)),
            dma((xcount,)),
            dma((hcount, 2)),
            dma((hcount, 2)),
            dma((hcount, 2)),
            dma((hcount, 2)),
            dma((xcount, blocks)),
            dma((xcount, blocks)),
        ],
        compiler_params=pltpu.CompilerParams(
            collective_id=0, has_side_effects=True, vmem_limit_bytes=60 * 1024 * 1024
        ),
        name="sweep_attention",
    )(
        queries,
        query_gain.reshape(1, width),
        cache_keys,
        cache_values,
        finished_keys,
        finished_values,
        new_keys,
        new_values,
        out_weight,
        time_weight,
        owner,
        step,
    )
    if aligned:
        return result
    summed = lax.psum_scatter(result, "head", scatter_dimension=1, tiled=True)
    half = freq // 2
    frequency = jnp.exp(-jnp.log(10000.0) * jnp.arange(half, dtype=F32) / half)
    phases = step[0].astype(F32) * frequency
    embedding = jnp.concatenate([jnp.cos(phases), jnp.sin(phases)])
    time_gate = 1.0 + jnp.dot(embedding, time_weight, precision=lax.Precision.HIGHEST)
    return (time_gate * summed).astype(BF16)


def solution(mesh):
    in_specs = (
        P(("grp", "seq"), "head"),
        P("head"),
        P(("grp", "slab"), "head"),
        P(("grp", "slab"), "head"),
        P(("grp", "slab", "seq"), "head"),
        P(("grp", "slab", "seq"), "head"),
        P(("grp", "slab", "seq"), "head"),
        P(("grp", "slab", "seq"), "head"),
        P("head", "slab"),
        P(None, ("slab", "head")),
        P("grp"),
        P("grp"),
    )
    out_specs = P(("grp", "seq"), ("slab", "head"))
    sizes = (mesh.shape["slab"], mesh.shape["head"], mesh.shape["seq"])
    return jax.shard_map(
        functools.partial(local, sizes),
        mesh=mesh,
        in_specs=in_specs,
        out_specs=out_specs,
        check_vma=False,
    )
```

time: 241 us -> 62.5 us (0.26)
  waiting for transfers between devices: 131 us -> 0 us
  Pallas kernels: 0 us -> 58 us
  blocking collectives: 29.2 us -> 0 us
  matrix products: 25.7 us -> 0 us
  local copies, waits for them, and re-layouts: 23.4 us -> 3.04 us
  other arithmetic: 15.2 us -> 0 us
  between operations: 14.9 us -> 1.31 us
    reduce_scatter x2 -> x0, waiting for transfers between devices: 73.1 us -> none  [the longest x1 51.8 us: local(): lax.psum_scatter(partial_value * factor[:, :, None], 'slab', scatter_dime...]
    pallas_call x0 -> x1, Pallas kernels: none -> 58 us  [local(): pl.pallas_call(functools.partial(kernel, sizes, aligned), out_shape=jax.S...]
    all_gather x3 -> x0, waiting for transfers between devices: 42.9 us -> none  [the longest x1 32.2 us: local(): attended = lax.all_gather(row_share, 'slab', axis=1, tiled=True)]
    dot_general x6 -> x0, matrix products: 25.7 us -> none  [the longest x2 11.8 us: local(): jnp.einsum('hrk,khd->hrd', raw_weights.astype(jnp.bfloat16), value_heads,...]
    pmax x1 -> x0, blocking collectives: 18.7 us -> none  [local(): global_top = lax.pmax(row_top, 'slab')]
    unnamed x7 -> x0, waiting for transfers between devices: 15.2 us -> none
    all_gather x4 -> x0, local copies, waits for them, and re-layouts: 11 us -> none  [the longest x1 4.41 us: local(): lax.all_gather(finished_values, ('slab', 'seq'), axis=0, tiled=True)]
    unnamed x19 -> x1, local copies, waits for them, and re-layouts: 12.4 us -> 1.73 us
  transfers between devices with their start and end apart: 6 -> 0, of which waited for: 5 -> 0; matrix products, arithmetic and copies ran while one was open for 16% -> 0% of each run, Pallas kernels for 0% -> 0%
where the time goes in v1:
time: 62.5 us; the launch traced here: 62.3 us
  Pallas kernels  58 us (93%)
  local copies, waits for them, and re-layouts  3.04 us (5%)
  between operations  1.31 us (2%)
    pallas_call x1, Pallas kernels, local(): pl.pallas_call(functools.partial(kernel, sizes, aligned), out_shape=jax.S...  58 us
    unnamed x1, local copies, waits for them, and re-layouts  1.73 us
    reshape x1, local copies, waits for them, and re-layouts, local(): query_gain.reshape(1, width)  1.31 us

profile of v1, /device:TPU:0, one launch (start us, length us, event | category | flops | bytes accessed | tf_op | source)
XLA Modules:
  0.0 62.3 jit_solution(7632332401144352142)
XLA Ops:
  1.3 1.3 %reshape.3.gain_ref = f32[1,2560]{1,0:T(1,128)} reshape(f32[2560]{0:T(1024)} %param.13) | data formatting | bytes 20480 | tf_op jit(solution)/shard_map/reshape | solution.py:459
  2.6 58.0 %sweep_attention.1 = bf16[256,640]{1,0:T(8,128)(2,1)} custom-call(bf16[256,2560]{1,0:T(8,128)(2,1)} %q_ref.1, f32[1,2560]{1,0:T(1,128)} %reshape.3.gain_ref, bf16[512,2560]{1,0:T(8,128)(2,1)} %ck_ref.1, bf16[512,2560]{1,0:T(8,128)(2,1)} %cv_ref.1, bf16[64,2560]{1,0:T(8,128)(2,1)} %fk_ref.1, bf16[64,2560]{1,0:T(8,128)(2,1)} %fv_ref.1, ...), custom_call_target="tpu_custom_call" | custom-call | tf_op jit(solution)/shard_map/sweep_attention/pallas_call | solution.py:407
  60.6 1.7 %copy.16 = bf16[256,640]{1,0:T(8,128)(2,1)} copy(bf16[256,640]{1,0:T(8,128)(2,1)} %sweep_attention.1) | data formatting | bytes 655360

commit v2 on v1

v2 whole, which is shorter than its diff:
```python
import functools
import math

import jax
import jax.numpy as jnp
from jax import lax
from jax.experimental import pallas as pl
from jax.experimental.pallas import tpu as pltpu
from jax.sharding import PartitionSpec as P

HEADS = 40
HD = 128
EPSILON = 1e-06
LOW = -1e30
LAG = 4
MESH = pl.DeviceIdType.MESH
F32 = jnp.float32
BF16 = jnp.bfloat16


def kernel(
    dims,
    aligned,
    q_ref,
    gain_ref,
    ck_ref,
    cv_ref,
    fk_ref,
    fv_ref,
    nk_ref,
    nv_ref,
    w_ref,
    tw_ref,
    owner_ref,
    step_ref,
    out_ref,
    q,
    qg,
    gain,
    kc,
    vc,
    kf,
    vf,
    w,
    tw,
    squares,
    scale,
    own_o,
    own_s,
    pre_o,
    pre_s,
    suf_o,
    suf_s,
    right_o,
    right_s,
    left_o,
    left_s,
    att,
    acc,
    gate,
    xs,
    xr,
    load_sem,
    fresh_sem,
    fresh_send,
    fresh_recv,
    sq_send,
    sq_recv,
    right_send,
    right_recv,
    left_send,
    left_recv,
    x_send,
    x_recv,
):
    n, heads_n, seq_n = dims
    rows, width = q_ref.shape
    hcount = width // HD
    z = lax.axis_index("slab")
    hx = lax.axis_index("head")
    sq = lax.axis_index("seq")

    groups = rows // HD
    chunks = groups * hcount
    loads = [
        pltpu.make_async_copy(src, dst, load_sem.at[i])
        for i, (src, dst) in enumerate(
            [(q_ref, q), (gain_ref, gain), (ck_ref, kc), (cv_ref, vc), (w_ref, w), (tw_ref, tw)]
        )
    ]
    loads[0].start()
    loads[1].start()
    barrier = pltpu.get_barrier_semaphore()
    for d in range(1, seq_n):
        pl.semaphore_signal(
            barrier, inc=1, device_id={"seq": lax.rem(sq + d, seq_n)}, device_id_type=MESH
        )
    for d in range(1, heads_n):
        pl.semaphore_signal(
            barrier, inc=1, device_id={"head": lax.rem(hx + d, heads_n)}, device_id_type=MESH
        )

    @pl.when(z > 0)
    def _():
        pl.semaphore_signal(barrier, inc=1, device_id={"slab": z - 1}, device_id_type=MESH)

    @pl.when(z < n - 1)
    def _():
        pl.semaphore_signal(barrier, inc=1, device_id={"slab": z + 1}, device_id_type=MESH)

    def clear(o_ref, s_ref):
        o_ref[...] = jnp.zeros_like(o_ref)
        s_ref[:, 0:1, :] = jnp.full((chunks, 1, HD), LOW, F32)
        s_ref[:, 1:2, :] = jnp.zeros((chunks, 1, HD), F32)

    @pl.when(z == 0)
    def _():
        clear(pre_o, pre_s)

    @pl.when(z == n - 1)
    def _():
        clear(suf_o, suf_s)

    ends = (z == 0).astype(jnp.int32) + (z == n - 1).astype(jnp.int32)
    pl.semaphore_wait(barrier, seq_n - 1 + heads_n - 1 + 2 - ends)

    fresh_src = [(fk_ref, kf, 0), (nk_ref, kf, 1), (fv_ref, vf, 0), (nv_ref, vf, 1)]
    fresh_remote = []
    for d in range(1, seq_n):
        for i, (src, dst, part) in enumerate(fresh_src):
            c = pltpu.make_async_remote_copy(
                src_ref=src,
                dst_ref=dst.at[sq, part],
                send_sem=fresh_send.at[d - 1, i],
                recv_sem=fresh_recv.at[d - 1, i],
                device_id={"seq": lax.rem(sq + d, seq_n)},
                device_id_type=MESH,
            )
            c.start()
            fresh_remote.append(c)

    loads[0].wait()
    loads[1].wait()
    loads[5].start()
    loads[2].start()
    loads[3].start()
    fresh_local = []
    for i, (src, dst, part) in enumerate(fresh_src):
        c = pltpu.make_async_copy(src, dst.at[sq, part], fresh_sem.at[i])
        c.start()
        fresh_local.append(c)
    loads[4].start()

    def squares_step(h, total):
        cols = pl.ds(pl.multiple_of(h * HD, HD), HD)
        x = q[:, cols].astype(F32)
        qg[:, cols] = (x * gain[cols][None, :]).astype(BF16)
        return total + x * x

    total = lax.fori_loop(0, hcount, squares_step, jnp.zeros((rows, HD), F32))
    row_total = jnp.sum(total.T, axis=0, keepdims=True)
    squares[hx] = jnp.broadcast_to(row_total, (8, rows))
    loads[5].wait()
    sq_copies = []
    for d in range(1, heads_n):
        c = pltpu.make_async_remote_copy(
            src_ref=squares.at[hx],
            dst_ref=squares.at[hx],
            send_sem=sq_send.at[d - 1],
            recv_sem=sq_recv.at[d - 1],
            device_id={"head": lax.rem(hx + d, heads_n)},
            device_id_type=MESH,
        )
        c.start()
        sq_copies.append(c)
    if aligned:
        half = tw.shape[0] // 2
        j = lax.broadcasted_iota(jnp.int32, (half, HD), 0).astype(F32)
        frequency = jnp.exp(F32(-math.log(10000.0)) * j / half)
        phases = jnp.full((half, HD), step_ref[0], jnp.int32).astype(F32) * frequency
        cos, sin = jnp.cos(phases), jnp.sin(phases)
        for c in range(tw.shape[1] // HD):
            cols = slice(c * HD, (c + 1) * HD)
            terms = tw[:half, cols] * cos + tw[half:, cols] * sin
            gate[:, cols] = 1.0 + jnp.sum(terms, axis=0, keepdims=True)

    for c in fresh_local + loads[2:4]:
        c.wait()
    for c in fresh_remote:
        c.wait_recv()
    for c in sq_copies:
        c.wait_recv()
    norm_total = jnp.sum(squares[...], axis=0)
    scale[...] = lax.rsqrt(norm_total / (HEADS * HD) + EPSILON) * (
        math.log2(math.e) / HD**0.5
    )
    def send(h, direction):
        if direction > 0:
            pairs, ss, rs = ((right_o, pre_o), (right_s, pre_s)), right_send, right_recv
        else:
            pairs, ss, rs = ((left_o, suf_o), (left_s, suf_s)), left_send, left_recv
        return [
            pltpu.make_async_remote_copy(
                src_ref=src.at[h],
                dst_ref=dst.at[h],
                send_sem=ss.at[h, i],
                recv_sem=rs.at[h, i],
                device_id={"slab": z + direction},
                device_id_type=MESH,
            )
            for i, (src, dst) in enumerate(pairs)
        ]

    pair = 2 if hcount % 2 == 0 else 1
    fresh_rows = seq_n * 2 * fk_ref.shape[0]
    lag_end = LAG * jnp.maximum(z, n - 1 - z)

    def combine(h, other_o, other_s, dest_o, dest_s):
        m_a, l_a = own_s[h, 0:1], own_s[h, 1:2]
        m_b, l_b = other_s[h, 0:1], other_s[h, 1:2]
        top = jnp.maximum(m_a, m_b)
        e_a, e_b = jnp.exp2(m_a - top), jnp.exp2(m_b - top)
        dest_o[h] = (own_o[h] * e_a + other_o[h].astype(F32) * e_b).astype(BF16)
        dest_s[h, 0:1] = top
        dest_s[h, 1:2] = l_a * e_a + l_b * e_b

    nt = (((1,), (1,)), ((), ()))
    tn = (((0,), (0,)), ((), ()))

    def attend(h):
        cols = pl.ds(pl.multiple_of(h * HD, HD), HD)
        penalty = jnp.where(
            jnp.full((1, rows), owner_ref[0], jnp.int32) == z, F32(LOW), F32(0.0)
        )
        q_head = qg[:, cols]
        s_row = scale[0:1]
        s_c = (
            lax.dot_general(kc[:, cols], q_head, nt, preferred_element_type=F32) * s_row
            + penalty
        )
        k_fresh = kf[:, :, :, cols].reshape(fresh_rows, HD)
        v_fresh = vf[:, :, :, cols].reshape(fresh_rows, HD)
        s_f = lax.dot_general(k_fresh, q_head, nt, preferred_element_type=F32) * s_row
        top = jnp.maximum(
            jnp.max(s_c, axis=0, keepdims=True), jnp.max(s_f, axis=0, keepdims=True)
        )
        p_c = jnp.exp2(s_c - top)
        p_f = jnp.exp2(s_f - top)
        mass = jnp.sum(p_c, axis=0, keepdims=True) + jnp.sum(p_f, axis=0, keepdims=True)
        o = lax.dot_general(
            vc[:, cols], p_c.astype(BF16), tn, preferred_element_type=F32
        ) + lax.dot_general(v_fresh, p_f.astype(BF16), tn, preferred_element_type=F32)
        for g in range(groups):
            part = slice(g * HD, (g + 1) * HD)
            own_s[g * hcount + h, 0:1] = top[:, part]
            own_s[g * hcount + h, 1:2] = mass[:, part]
            own_o[g * hcount + h] = o[:, part]

    def project(g, p):
        deep = pl.ds(pl.multiple_of(p * pair * HD, HD), pair * HD)
        term = lax.dot_general(att[g, deep, :], w[deep, :], tn, preferred_element_type=F32)

        @pl.when(p == 0)
        def _():
            acc[g] = term

        @pl.when(p > 0)
        def _():
            acc[g] += term

    def exchange(g):
        copies = []
        for d in range(1, heads_n):
            copies.append(
                pltpu.make_async_remote_copy(
                    src_ref=xs.at[d - 1, g],
                    dst_ref=xr.at[d - 1, g],
                    send_sem=x_send.at[d - 1, g],
                    recv_sem=x_recv.at[d - 1, g],
                    device_id={"head": lax.rem(hx + d, heads_n)},
                    device_id_type=MESH,
                )
            )
        return copies

    def exchange_start(g):
        cp = out_ref.shape[1]
        for d, c in enumerate(exchange(g)):
            peer = lax.rem(hx + d + 1, heads_n)
            cols = pl.ds(pl.multiple_of(peer * cp, HD), cp)
            xs[d, g] = acc[g, :, cols].astype(BF16)
            c.start()

    pairs = hcount // pair
    last = (groups - 1) * hcount
    attend(0)

    def body(t, carry):
        cp_ = t - LAG * z
        in_p = (cp_ >= 0) & (cp_ < chunks)
        cs = t - LAG * (n - 1 - z)
        in_s = (cs >= 0) & (cs < chunks)

        @pl.when(in_p & (z > 0))
        def _():
            for c in send(cp_, 1):
                c.wait_recv()

        @pl.when(in_p & (z < n - 1))
        def _():
            combine(cp_, pre_o, pre_s, right_o, right_s)

        @pl.when(in_s & (z < n - 1))
        def _():
            for c in send(cs, -1):
                c.wait_recv()

        @pl.when(in_s & (z > 0))
        def _():
            combine(cs, suf_o, suf_s, left_o, left_s)

        f = t - lag_end

        @pl.when((f >= 0) & (f < chunks))
        def _():
            m_a, m_b, m_c = own_s[f, 0:1], pre_s[f, 0:1], suf_s[f, 0:1]
            top = jnp.maximum(m_a, jnp.maximum(m_b, m_c))
            e_a, e_b, e_c = jnp.exp2(m_a - top), jnp.exp2(m_b - top), jnp.exp2(m_c - top)
            mass = own_s[f, 1:2] * e_a + pre_s[f, 1:2] * e_b + suf_s[f, 1:2] * e_c
            total_o = (
                own_o[f] * e_a + pre_o[f].astype(F32) * e_b + suf_o[f].astype(F32) * e_c
            )
            h = lax.rem(f, hcount)
            att[f // hcount, pl.ds(pl.multiple_of(h * HD, HD), HD), :] = (
                total_o / mass
            ).astype(BF16)

        @pl.when(in_p & (z < n - 1))
        def _():
            for c in send(cp_, 1):
                c.start()

        @pl.when(in_s & (z > 0))
        def _():
            for c in send(cs, -1):
                c.start()

        @pl.when(t + 1 < hcount)
        def _():
            attend(t + 1)

        @pl.when(f == last)
        def _():
            loads[4].wait()

        for g in range(groups - 1):

            @pl.when((f >= last) & (f < last + pairs))
            def _(g=g):
                project(g, f - last)

            if aligned:

                @pl.when(f == last + pairs - 1)
                def _(g=g):
                    exchange_start(g)

        done = f - last + 1

        @pl.when((done > 0) & (done <= hcount) & (lax.rem(done, pair) == 0))
        def _():
            project(groups - 1, done // pair - 1)

        return carry

    lax.fori_loop(0, chunks + LAG * (n - 1), body, 0)

    if aligned:
        cp = out_ref.shape[1]
        mine = pl.ds(pl.multiple_of(hx * cp, HD), cp)
        exchange_start(groups - 1)
        for g in range(groups):
            summed = acc[g, :, mine]
            for d, c in enumerate(exchange(g)):
                c.wait_recv()
                summed = summed + xr[d, g].astype(F32)
            out_ref[g * HD : (g + 1) * HD, :] = (summed * gate[...]).astype(out_ref.dtype)
        for g in range(groups):
            for c in exchange(g):
                c.wait_send()
    else:
        for g in range(groups):
            out_ref[g * HD : (g + 1) * HD, :] = acc[g]

    for c in fresh_remote + sq_copies:
        c.wait_send()

    def drain(h, carry):
        @pl.when(z < n - 1)
        def _():
            for c in send(h, 1):
                c.wait_send()

        @pl.when(z > 0)
        def _():
            for c in send(h, -1):
                c.wait_send()

        return carry

    lax.fori_loop(0, chunks, drain, 0)


def local(sizes, *args):
    (
        queries,
        query_gain,
        cache_keys,
        cache_values,
        finished_keys,
        finished_values,
        new_keys,
        new_values,
        out_weight,
        time_weight,
        owner,
        step,
    ) = args
    n, heads_n, seq_n = sizes
    rows, width = queries.shape
    hcount = width // HD
    cached, fresh = cache_keys.shape[0], finished_keys.shape[0]
    columns, cp = out_weight.shape[1], time_weight.shape[1]
    freq = time_weight.shape[0]
    aligned = cp % HD == 0
    any_spec = pl.BlockSpec(memory_space=pl.ANY)
    smem = pl.BlockSpec(memory_space=pltpu.SMEM)
    vmem = pl.BlockSpec(memory_space=pltpu.VMEM)
    dma = pltpu.SemaphoreType.DMA
    xcount = max(heads_n - 1, 1)
    groups = rows // HD
    chunks = groups * hcount
    stat = (chunks, 2, HD)
    part = (chunks, HD, HD)
    result = pl.pallas_call(
        functools.partial(kernel, sizes, aligned),
        out_shape=jax.ShapeDtypeStruct(
            (rows, cp if aligned else columns), BF16 if aligned else F32
        ),
        in_specs=[any_spec] * 10 + [smem] * 2,
        out_specs=vmem,
        scratch_shapes=[
            pltpu.VMEM((rows, width), BF16),
            pltpu.VMEM((rows, width), BF16),
            pltpu.VMEM((width,), F32),
            pltpu.VMEM((cached, width), BF16),
            pltpu.VMEM((cached, width), BF16),
            pltpu.VMEM((seq_n, 2, fresh, width), BF16),
            pltpu.VMEM((seq_n, 2, fresh, width), BF16),
            pltpu.VMEM((width, columns), BF16),
            pltpu.VMEM((freq, cp), F32),
            pltpu.VMEM((heads_n, 8, rows), F32),
            pltpu.VMEM((8, rows), F32),
            pltpu.VMEM(part, F32),
            pltpu.VMEM(stat, F32),
            pltpu.VMEM(part, BF16),
            pltpu.VMEM(stat, F32),
            pltpu.VMEM(part, BF16),
            pltpu.VMEM(stat, F32),
            pltpu.VMEM(part, BF16),
            pltpu.VMEM(stat, F32),
            pltpu.VMEM(part, BF16),
            pltpu.VMEM(stat, F32),
            pltpu.VMEM((groups, width, HD), BF16),
            pltpu.VMEM((groups, HD, columns), F32),
            pltpu.VMEM((1, cp), F32),
            pltpu.VMEM((xcount, groups, HD, cp), BF16),
            pltpu.VMEM((xcount, groups, HD, cp), BF16),
            dma((6,)),
            dma((4,)),
            dma((max(seq_n - 1, 1), 4)),
            dma((max(seq_n - 1, 1), 4)),
            dma((xcount,)),
            dma((xcount,)),
            dma((chunks, 2)),
            dma((chunks, 2)),
            dma((chunks, 2)),
            dma((chunks, 2)),
            dma((xcount, groups)),
            dma((xcount, groups)),
        ],
        compiler_params=pltpu.CompilerParams(
            collective_id=0, has_side_effects=True, vmem_limit_bytes=60 * 1024 * 1024
        ),
        name="sweep_attention",
    )(
        queries,
        query_gain,
        cache_keys,
        cache_values,
        finished_keys,
        finished_values,
        new_keys,
        new_values,
        out_weight,
        time_weight,
        owner,
        step,
    )
    if aligned:
        return result
    summed = lax.psum_scatter(result, "head", scatter_dimension=1, tiled=True)
    half = freq // 2
    frequency = jnp.exp(-jnp.log(10000.0) * jnp.arange(half, dtype=F32) / half)
    phases = step[0].astype(F32) * frequency
    embedding = jnp.concatenate([jnp.cos(phases), jnp.sin(phases)])
    time_gate = 1.0 + jnp.dot(embedding, time_weight, precision=lax.Precision.HIGHEST)
    return (time_gate * summed).astype(BF16)


def solution(mesh):
    in_specs = (
        P(("grp", "seq"), "head"),
        P("head"),
        P(("grp", "slab"), "head"),
        P(("grp", "slab"), "head"),
        P(("grp", "slab", "seq"), "head"),
        P(("grp", "slab", "seq"), "head"),
        P(("grp", "slab", "seq"), "head"),
        P(("grp", "slab", "seq"), "head"),
        P("head", "slab"),
        P(None, ("slab", "head")),
        P("grp"),
        P("grp"),
    )
    out_specs = P(("grp", "seq"), ("slab", "head"))
    sizes = (mesh.shape["slab"], mesh.shape["head"], mesh.shape["seq"])
    return jax.shard_map(
        functools.partial(local, sizes),
        mesh=mesh,
        in_specs=in_specs,
        out_specs=out_specs,
        check_vma=False,
    )
```

time: 62.5 us -> 62.5 us (level)
  local copies, waits for them, and re-layouts: 3.04 us -> 1.73 us
  Pallas kernels: 58 us -> 59.3 us
    pallas_call x1, Pallas kernels: 58 us -> 59.3 us  [local(): pl.pallas_call(functools.partial(kernel, sizes, aligned), out_shape=jax.S...]
    reshape x1 -> x0, local copies, waits for them, and re-layouts: 1.31 us -> none  [local(): query_gain.reshape(1, width)]
where the time goes in v2:
time: 62.5 us; the launch traced here: 62.3 us
  Pallas kernels  59.3 us (95%)
  local copies, waits for them, and re-layouts  1.73 us (3%)
  between operations  1.3 us (2%)
    pallas_call x1, Pallas kernels, local(): pl.pallas_call(functools.partial(kernel, sizes, aligned), out_shape=jax.S...  59.3 us
    unnamed x1, local copies, waits for them, and re-layouts  1.73 us

profile of v2, /device:TPU:0, one launch (start us, length us, event | category | flops | bytes accessed | tf_op | source)
XLA Modules:
  0.0 62.3 jit_solution(2597030257659805673)
XLA Ops:
  1.3 59.3 %sweep_attention.1 = bf16[256,640]{1,0:T(8,128)(2,1)} custom-call(bf16[256,2560]{1,0:T(8,128)(2,1)} %q_ref.1, f32[2560]{0:T(1024)} %gain_ref.1, bf16[512,2560]{1,0:T(8,128)(2,1)} %ck_ref.1, bf16[512,2560]{1,0:T(8,128)(2,1)} %cv_ref.1, bf16[64,2560]{1,0:T(8,128)(2,1)} %fk_ref.1, bf16[64,2560]{1,0:T(8,128)(2,1)} %fv_ref.1, bf16[64,2560]{1,0:T(8,128)(2,1)} %nk_ref.1, ...), custom_call_target="tpu_custom_call" | custom-call | tf_op jit(solution)/shard_map/sweep_attention/pallas_call | solution.py:445
  60.6 1.7 %copy.16 = bf16[256,640]{1,0:T(8,128)(2,1)} copy(bf16[256,640]{1,0:T(8,128)(2,1)} %sweep_attention.1) | data formatting | bytes 655360

commit v3 on v2

--- a/solution.py
+++ b/solution.py
@@ -12,7 +12,7 @@
 HD = 128
 EPSILON = 1e-06
 LOW = -1e30
-LAG = 4
+LAG = 5
 MESH = pl.DeviceIdType.MESH
 F32 = jnp.float32
 BF16 = jnp.bfloat16
@@ -125,19 +125,22 @@
     pl.semaphore_wait(barrier, seq_n - 1 + heads_n - 1 + 2 - ends)
 
     fresh_src = [(fk_ref, kf, 0), (nk_ref, kf, 1), (fv_ref, vf, 0), (nv_ref, vf, 1)]
-    fresh_remote = []
-    for d in range(1, seq_n):
-        for i, (src, dst, part) in enumerate(fresh_src):
-            c = pltpu.make_async_remote_copy(
-                src_ref=src,
-                dst_ref=dst.at[sq, part],
-                send_sem=fresh_send.at[d - 1, i],
-                recv_sem=fresh_recv.at[d - 1, i],
-                device_id={"seq": lax.rem(sq + d, seq_n)},
-                device_id_type=MESH,
-            )
-            c.start()
-            fresh_remote.append(c)
+    first = max(hcount // 5, 1) * HD
+    cuts = [slice(0, first), slice(first, width)]
+    fresh_remote = [[], []]
+    for k, cols in enumerate(cuts):
+        for d in range(1, seq_n):
+            for i, (src, dst, part) in enumerate(fresh_src):
+                c = pltpu.make_async_remote_copy(
+                    src_ref=src.at[:, cols],
+                    dst_ref=dst.at[sq, part, :, cols],
+                    send_sem=fresh_send.at[d - 1, k, i],
+                    recv_sem=fresh_recv.at[d - 1, k, i],
+                    device_id={"seq": lax.rem(sq + d, seq_n)},
+                    device_id_type=MESH,
+                )
+                c.start()
+                fresh_remote[k].append(c)
 
     loads[0].wait()
     loads[1].wait()
@@ -186,7 +189,7 @@
 
     for c in fresh_local + loads[2:4]:
         c.wait()
-    for c in fresh_remote:
+    for c in fresh_remote[0]:
         c.wait_recv()
     for c in sq_copies:
         c.wait_recv()
@@ -345,6 +348,11 @@
             for c in send(cs, -1):
                 c.start()
 
+        @pl.when(t + 1 == first // HD)
+        def _():
+            for c in fresh_remote[1]:
+                c.wait_recv()
+
         @pl.when(t + 1 < hcount)
         def _():
             attend(t + 1)
@@ -392,7 +400,7 @@
         for g in range(groups):
             out_ref[g * HD : (g + 1) * HD, :] = acc[g]
 
-    for c in fresh_remote + sq_copies:
+    for c in fresh_remote[0] + fresh_remote[1] + sq_copies:
         c.wait_send()
 
     def drain(h, carry):
@@ -478,8 +486,8 @@
             pltpu.VMEM((xcount, groups, HD, cp), BF16),
             dma((6,)),
             dma((4,)),
-            dma((max(seq_n - 1, 1), 4)),
-            dma((max(seq_n - 1, 1), 4)),
+            dma((max(seq_n - 1, 1), 2, 4)),
+            dma((max(seq_n - 1, 1), 2, 4)),
             dma((xcount,)),
             dma((xcount,)),
             dma((chunks, 2)),

time: 62.5 us -> 60.5 us (0.968)
  Pallas kernels: 59.3 us -> 57.3 us
    pallas_call x1, Pallas kernels: 59.3 us -> 57.3 us  [local(): pl.pallas_call(functools.partial(kernel, sizes, aligned), out_shape=jax.S...]
where the time goes in v3:
time: 60.5 us; the launch traced here: 60.3 us
  Pallas kernels  57.3 us (95%)
  local copies, waits for them, and re-layouts  1.73 us (3%)
  between operations  1.3 us (2%)
    pallas_call x1, Pallas kernels, local(): pl.pallas_call(functools.partial(kernel, sizes, aligned), out_shape=jax.S...  57.3 us
    unnamed x1, local copies, waits for them, and re-layouts  1.73 us

profile of v3, /device:TPU:0, one launch (start us, length us, event | category | flops | bytes accessed | tf_op | source)
XLA Modules:
  0.0 60.3 jit_solution(14135727846626804923)
XLA Ops:
  1.3 57.3 %sweep_attention.1 = bf16[256,640]{1,0:T(8,128)(2,1)} custom-call(bf16[256,2560]{1,0:T(8,128)(2,1)} %q_ref.1, f32[2560]{0:T(1024)} %gain_ref.1, bf16[512,2560]{1,0:T(8,128)(2,1)} %ck_ref.1, bf16[512,2560]{1,0:T(8,128)(2,1)} %cv_ref.1, bf16[64,2560]{1,0:T(8,128)(2,1)} %fk_ref.1, bf16[64,2560]{1,0:T(8,128)(2,1)} %fv_ref.1, bf16[64,2560]{1,0:T(8,128)(2,1)} %nk_ref.1, ...), custom_call_target="tpu_custom_call" | custom-call | tf_op jit(solution)/shard_map/sweep_attention/pallas_call | solution.py:453
  58.6 1.7 %copy.16 = bf16[256,640]{1,0:T(8,128)(2,1)} copy(bf16[256,640]{1,0:T(8,128)(2,1)} %sweep_attention.1) | data formatting | bytes 655360
